TPU v7x, 32 devices: a 4x2x2 block of a 4x4x8 slice. The times are simulated.
32 devices in a mesh: dp: 4 (over y, z), ep: 8 (over x, core).
Axes of the slice: x: 4, y: 2, z: 2, core: 2. Of those that a mesh axis runs over, the one named last changes fastest.
The devices are a block of a 4x4x8 slice.
Arguments:
- tokens: bfloat16 [32, 2048, 2048], P(('dp', 'ep')), parts along dimension 0
- w_gate: bfloat16 [2048, 64], replicated
- expert_ids: int32 [32, 2048, 2], P(('dp', 'ep')), parts along dimension 0
- keep_second: int32 [32, 2048], P(('dp', 'ep')), parts along dimension 0
- w_in: bfloat16 [64, 2048, 1024], P('ep')
- w_out: bfloat16 [64, 1024, 2048], P('ep')
Outputs:
- output: bfloat16 [32, 2048, 2048], P(('dp', 'ep')), parts along dimension 0
There are 4 independent parts. A program takes and returns all parts, laid end to end along the dimension named above; an argument that names none is the same for every part.
All inputs are finite; a program needn't handle non-finite values.
Results may differ from a plain program's by a relative error of at most 0.001.
Values are sent between devices in bfloat16 or wider.
A program may use at most 768 MiB of HBM per device.

v0:
```python
import jax
import jax.numpy as jnp
from jax import lax
from jax.sharding import PartitionSpec as P


def build_routing(tokens, w_gate, expert_ids, keep_second, capacity):
    expert_count = w_gate.shape[1]
    logits = jnp.einsum("gsm,me->gse", tokens, w_gate, preferred_element_type=jnp.float32)
    gate_probs = jax.nn.softmax(logits, axis=-1)
    first_hot = jax.nn.one_hot(expert_ids[:, :, 0], expert_count, dtype=jnp.int32)
    second_hot = jax.nn.one_hot(expert_ids[:, :, 1], expert_count, dtype=jnp.int32) * keep_second[:, :, None]
    gate_first = jnp.sum(gate_probs * first_hot, axis=-1)
    gate_second = jnp.sum(gate_probs * second_hot, axis=-1)
    gate_total = gate_first + gate_second
    pos_first = jnp.sum((jnp.cumsum(first_hot, axis=1) - first_hot) * first_hot, axis=-1)
    second_base = jnp.cumsum(second_hot, axis=1) - second_hot + jnp.sum(first_hot, axis=1, keepdims=True)
    pos_second = jnp.sum(second_base * second_hot, axis=-1)
    slot_first = first_hot.astype(jnp.bfloat16)[:, :, :, None] * jax.nn.one_hot(pos_first, capacity, dtype=jnp.bfloat16)[:, :, None, :]
    slot_second = second_hot.astype(jnp.bfloat16)[:, :, :, None] * jax.nn.one_hot(pos_second, capacity, dtype=jnp.bfloat16)[:, :, None, :]
    dispatch = slot_first + slot_second
    weight_first = (gate_first / gate_total).astype(jnp.bfloat16)[:, :, None, None]
    weight_second = (gate_second / gate_total).astype(jnp.bfloat16)[:, :, None, None]
    combine = weight_first * slot_first + weight_second * slot_second
    return dispatch, combine


def solution(mesh):
    group_count = mesh.shape["ep"]

    def local_layer(tokens, w_gate, expert_ids, keep_second, w_in, w_out):
        token_count = tokens.shape[1]
        model_dim = tokens.shape[2]
        expert_count = w_gate.shape[1]
        local_experts = w_in.shape[0]
        capacity = 2 * token_count // expert_count
        dispatch, combine = build_routing(tokens, w_gate, expert_ids, keep_second, capacity)
        send_rows = jnp.einsum("gsec,gsm->ecm", dispatch, tokens, preferred_element_type=jnp.float32).astype(jnp.bfloat16)
        send_rows = send_rows.reshape(group_count, local_experts, capacity, model_dim)
        recv_rows = lax.all_to_all(send_rows, "ep", 0, 0, tiled=True)
        hidden = jax.nn.relu(jnp.einsum("gecm,emh->egch", recv_rows, w_in, preferred_element_type=jnp.float32)).astype(jnp.bfloat16)
        back_rows = jnp.einsum("egch,ehm->gecm", hidden, w_out, preferred_element_type=jnp.float32).astype(jnp.bfloat16)
        back_rows = lax.all_to_all(back_rows, "ep", 0, 0, tiled=True)
        back_rows = back_rows.reshape(expert_count, capacity, model_dim)
        mixed_rows = jnp.einsum("gsec,ecm->gsm", combine, back_rows, preferred_element_type=jnp.float32)
        return mixed_rows.astype(jnp.bfloat16)

    group_spec = P(("dp", "ep"))
    return jax.shard_map(local_layer, mesh=mesh, in_specs=(group_spec, P(), group_spec, group_spec, P("ep"), P("ep")), out_specs=group_spec, check_vma=False)
```

profile of v0, /device:TPU:81, one launch (start us, length us, event | category | flops | bytes accessed | tf_op | source)
XLA Modules:
  0.0 597.3 jit_solution(523881128974041496)
XLA Ops:
  0.0 0.0 copy-start
  0.0 0.8 fusion.48
  0.8 0.0 copy-start.9
  0.8 0.0 copy-start.11
  0.8 0.7 select_convert_fusion
  1.6 0.0 copy-start.1
  1.6 0.8 select_bitcast_fusion
  2.4 0.1 copy.34
  2.5 18.1 %reduce-window.16 = s32[1,64,16,128]{3,2,1,0:T(8,128)S(1)} reduce-window(s32[1,64,16,128]{3,2,1,0:T(8,128)S(1)} %bitcast.64, s32[]{:T(128)} %constant.14.clone.1), window={size=1x1x1x128 pad=0_0x0_0x0_0x127_0}, to_apply=%region_7.8 | reduce-window | flops 16646144 | bytes 1048580 | tf_op jit(solution)/shard_map/reduce-window.2
  20.6 0.2 slice.26
  20.8 0.1 reshape.436
  21.0 0.1 copy.33
  21.1 18.1 %reduce-window.14 = s32[1,64,16,128]{3,2,1,0:T(8,128)S(1)} reduce-window(s32[1,64,16,128]{3,2,1,0:T(8,128)S(1)} %bitcast.65, s32[]{:T(128)} %constant.14.clone.1), window={size=1x1x1x128 pad=0_0x0_0x0_0x127_0}, to_apply=%region_4.5 | reduce-window | flops 16646144 | bytes 1048580 | tf_op jit(solution)/shard_map/reduce-window
  39.2 0.2 slice.24
  39.4 0.1 reshape.431
  39.5 0.3 copy.25
  39.8 0.1 copy.26
  39.9 0.2 reduce-window.19
  40.0 0.2 broadcast.220
  40.2 0.1 reshape.439
  40.3 0.3 copy.23
  40.6 0.1 copy.24
  40.7 0.2 reduce-window.15
  40.9 0.2 broadcast.218
  41.1 0.1 reshape.434
  41.2 0.2 fusion.35
  41.4 0.9 fusion.41
  42.3 0.0 copy-start.3
  42.3 0.1 convert_convert_fusion
  42.5 0.6 copy-done.3
  43.0 0.1 copy-done.5
  43.1 0.1 copy-done.7
  43.2 6.1 %multiply_add_fusion = bf16[2048,64,64]{0,1,2:T(8,128)(2,1)} fusion(bf16[2048,64]{0,1:T(8,128)(2,1)S(1)} %fusion.43, bf16[2048,64]{0,1:T(8,128)(2,1)S(1)} %select_convert_fusion, bf16[2048,64]{0,1:T(8,128)(2,1)S(1)} %get-tuple-element.16, bf16[2048,64]{0,1:T(8,128)(2,1)S(1)} %get-tuple-element.15), kind=kLoop, calls=%fused_computation.4 | loop fusion | flops 25165824 | bytes 17825792 | tf_op jit(solution)/shard_map/add | solution.py:21
  49.3 0.0 copy-done.11
  49.3 45.2 %fusion.11 = bf16[64,64,2048]{2,1,0:T(8,128)(2,1)S(1)} fusion(bf16[2048,64,64]{0,1,2:T(8,128)(2,1)} %multiply_add_fusion, bf16[1,2048,2048]{2,1,0:T(8,128)(2,1)} %param.6), kind=kOutput, calls=%fused_computation.16 | convolution fusion | flops 34368126976 | bytes 41943040 | tf_op jit(solution)/shard_map/gsec,gsm->ecm/dot_general | solution.py:38
  94.6 189.3 %all_to_all.10 = bf16[8,8,64,2048]{3,2,1,0:T(8,128)(2,1)} all-to-all(bf16[8,8,64,2048]{3,2,1,0:T(8,128)(2,1)S(1)} %bitcast.63), channel_id=1, replica_groups=mesh['dp'=4,'ep'=8] {'ep'}, dimensions={0} | all-to-all | bytes 33554432 | tf_op jit(solution)/shard_map/all_to_all | solution.py:40
  283.9 31.4 %maximum_convert_fusion = bf16[8,8,64,1024]{3,2,1,0:T(8,128)(2,1)} fusion(bf16[8,2048,1024]{2,1,0:T(8,128)(2,1)} %param.10, bf16[8,8,64,2048]{3,2,1,0:T(8,128)(2,1)} %all_to_all.10), kind=kOutput, calls=%fused_computation.15 | convolution fusion | flops 17188257792 | bytes 58720256 | tf_op jit(solution)/shard_map/gecm,emh->egch/dot_general | solution.py:41
  315.3 26.4 %convert_bitcast_fusion = bf16[8,8,64,2048]{3,2,0,1:T(8,128)(2,1)} fusion(bf16[8,8,64,1024]{3,2,1,0:T(8,128)(2,1)} %maximum_convert_fusion, bf16[8,1024,2048]{2,1,0:T(8,128)(2,1)} %param.11), kind=kOutput, calls=%fused_computation.14 | convolution fusion | flops 17188257792 | bytes 58720256 | tf_op jit(solution)/shard_map/egch,ehm->gecm/dot_general | solution.py:42
  341.6 14.1 %copy.29 = bf16[8,8,64,2048]{3,2,1,0:T(8,128)(2,1)} copy(bf16[8,8,64,2048]{3,2,0,1:T(8,128)(2,1)} %convert_bitcast_fusion) | data formatting | bytes 33554432 | tf_op jit(solution)/shard_map/convert_element_type | solution.py:42
  355.7 0.0 copy-start.4
  355.8 0.0 copy-start.6
  355.8 0.0 copy-start.8
  355.8 6.8 %all-to-all-start.1 = ((bf16[8,8,64,2048]{3,2,1,0:T(8,128)(2,1)}), bf16[8,8,64,2048]{3,2,1,0:T(8,128)(2,1)}, u32[]{:S(2)}, u32[]{:S(2)}) async-start(bf16[8,8,64,2048]{3,2,1,0:T(8,128)(2,1)} %copy.29), calls=%async_computation.1 | async-start | bytes 33554432 | tf_op jit(solution)/shard_map/all_to_all | solution.py:43
  362.6 6.0 %fusion.49 = (f32[2048]{0:T(1024)S(1)}, f32[2048,64]{0,1:T(8,128)S(1)}) fusion(bf16[2048,64]{0,1:T(8,128)(2,1)S(1)} %copy-done, bf16[1,2048,2048]{2,1,0:T(8,128)(2,1)} %param.6), kind=kOutput, calls=%fused_computation.63 | convolution fusion | flops 536999936 | bytes 9183232 | tf_op jit(solution)/shard_map/gsm,me->gse/dot_general | solution.py:9
  368.7 0.1 fusion.45
  368.8 0.2 fusion.39
  369.0 177.0 %all-to-all-done.1 = bf16[8,8,64,2048]{3,2,1,0:T(8,128)(2,1)} async-done(((bf16[8,8,64,2048]{3,2,1,0:T(8,128)(2,1)}), bf16[8,8,64,2048]{3,2,1,0:T(8,128)(2,1)}, u32[]{:S(2)}, u32[]{:S(2)}) %all-to-all-start.1) | async-done | bytes 16777248 | tf_op jit(solution)/shard_map/all_to_all | solution.py:43
  546.1 51.2 %fusion.20 = bf16[1,2048,2048]{2,1,0:T(8,128)(2,1)} fusion(bf16[64,64,2048]{2,1,0:T(8,128)(2,1)} %bitcast.19, bf16[2048,64]{0,1:T(8,128)(2,1)S(1)} %copy-done.4, bf16[2048,64]{0,1:T(8,128)(2,1)S(1)} %copy-done.2, bf16[2048]{0:T(1024)(128)(2,1)S(1)} %get-tuple-element.10, bf16[2048,64]{0,1:T(8,128)(2,1)S(1)} %copy-done.8, ...), kind=kOutput, calls=%fused_computation.17 | convolution fusion | flops 34405875712 | bytes 26222592 | tf_op jit(solution)/shard_map/gsec,ecm->gsm/dot_general | solution.py:45
  (21 shorter events, 0.1 us)
Async XLA Ops:
  0.0 362.6 %copy-start = (bf16[2048,64]{0,1:T(8,128)(2,1)S(1)}, bf16[2048,64]{0,1:T(8,128)(2,1)}, u32[]{:S(2)}) copy-start(bf16[2048,64]{0,1:T(8,128)(2,1)} %param.7) | copy-start | bytes 786436
  0.8 48.5 %copy-start.9 = (s32[1,2048,1]{1,2,0:T(1,128)}, s32[1,2048,1]{1,2,0:T(1,128)S(1)}, u32[]{:S(2)}) copy-start(s32[1,2048,1]{1,2,0:T(1,128)S(1)} %get-tuple-element.11) | copy-start | bytes 24580
  0.8 48.5 %copy-start.11 = (s32[1,2048,1]{1,2,0:T(1,128)}, s32[1,2048,1]{1,2,0:T(1,128)S(1)}, u32[]{:S(2)}) copy-start(s32[1,2048,1]{1,2,0:T(1,128)S(1)} %get-tuple-element.12) | copy-start | bytes 24580
  1.6 47.7 %copy-start.1 = (bf16[2048,64]{0,1:T(8,128)(2,1)}, bf16[2048,64]{0,1:T(8,128)(2,1)S(1)}, u32[]{:S(2)}) copy-start(bf16[2048,64]{0,1:T(8,128)(2,1)S(1)} %select_convert_fusion) | copy-start | bytes 786436
  42.3 0.7 copy-start.3
  42.4 0.7 copy-start.5
  42.4 0.8 copy-start.7
  355.7 13.0 %copy-start.10 = (s32[1,2048,1]{1,2,0:T(1,128)S(1)}, s32[1,2048,1]{1,2,0:T(1,128)}, u32[]{:S(2)}) copy-start(s32[1,2048,1]{1,2,0:T(1,128)} %copy-done.9) | copy-start | bytes 24580
  355.7 13.0 %copy-start.12 = (s32[1,2048,1]{1,2,0:T(1,128)S(1)}, s32[1,2048,1]{1,2,0:T(1,128)}, u32[]{:S(2)}) copy-start(s32[1,2048,1]{1,2,0:T(1,128)} %copy-done.11) | copy-start | bytes 24580
  355.7 13.0 %copy-start.13 = (s32[1,2048]{1,0:T(1,128)S(1)}, s32[1,2048]{1,0:T(1,128)}, u32[]{:S(2)}) copy-start(s32[1,2048]{1,0:T(1,128)} %param.9) | copy-start | bytes 24580
  355.7 190.4 %copy-start.2 = (bf16[2048,64]{0,1:T(8,128)(2,1)S(1)}, bf16[2048,64]{0,1:T(8,128)(2,1)}, u32[]{:S(2)}) copy-start(bf16[2048,64]{0,1:T(8,128)(2,1)} %copy-done.1) | copy-start | bytes 786436
  355.7 190.3 %copy-start.4 = (bf16[2048,64]{0,1:T(8,128)(2,1)S(1)}, bf16[2048,64]{0,1:T(8,128)(2,1)}, u32[]{:S(2)}) copy-start(bf16[2048,64]{0,1:T(8,128)(2,1)} %copy-done.3) | copy-start | bytes 786436
  355.8 190.3 %copy-start.6 = (bf16[2048,64]{0,1:T(8,128)(2,1)S(1)}, bf16[2048,64]{0,1:T(8,128)(2,1)}, u32[]{:S(2)}) copy-start(bf16[2048,64]{0,1:T(8,128)(2,1)} %copy-done.5) | copy-start | bytes 786436
  355.8 190.3 %copy-start.8 = (bf16[2048,64]{0,1:T(8,128)(2,1)S(1)}, bf16[2048,64]{0,1:T(8,128)(2,1)}, u32[]{:S(2)}) copy-start(bf16[2048,64]{0,1:T(8,128)(2,1)} %copy-done.7) | copy-start | bytes 786436
  355.8 190.3 %all-to-all-start.1 = ((bf16[8,8,64,2048]{3,2,1,0:T(8,128)(2,1)}), bf16[8,8,64,2048]{3,2,1,0:T(8,128)(2,1)}, u32[]{:S(2)}, u32[]{:S(2)}) async-start(bf16[8,8,64,2048]{3,2,1,0:T(8,128)(2,1)} %copy.29), calls=%async_computation.1 | async-start | bytes 33554432 | tf_op jit(solution)/shard_map/all_to_all | solution.py:43
where the time goes:
time: 598 us; the launch traced here: 597 us
  blocking collectives  189 us (32%)
  waiting for transfers between devices  177 us (30%)
  matrix products  160 us (27%)
  other arithmetic  45.8 us (8%)
  local copies, waits for them, and re-layouts  17.8 us (3%)
  starting transfers between devices  6.82 us (1%)
    all_to_all x1, blocking collectives, local_layer(): recv_rows = lax.all_to_all(send_rows, 'ep', 0, 0, tiled=True)  189 us
    all_to_all x1, waiting for transfers between devices, local_layer(): back_rows = lax.all_to_all(back_rows, 'ep', 0, 0, tiled=True)  177 us
    dot_general x1, matrix products, local_layer(): jnp.einsum('gsec,ecm->gsm', combine, back_rows, preferred_element_type=jn...  51.2 us
    dot_general x1, matrix products, local_layer(): jnp.einsum('gsec,gsm->ecm', dispatch, tokens, preferred_element_type=jnp....  45.2 us
    another operation x4, other arithmetic  36.6 us
    dot_general x1, matrix products, local_layer(): jnp.einsum('gecm,emh->egch', recv_rows, w_in, preferred_element_type=jnp....  31.4 us
    dot_general x1, matrix products, local_layer(): jnp.einsum('egch,ehm->gecm', hidden, w_out, preferred_element_type=jnp.fl...  26.4 us
    convert_element_type x1, local copies, waits for them, and re-layouts, local_layer(): jnp.einsum('egch,ehm->gecm', hidden, w_out, preferred_element_type=jnp.fl...  14.1 us
  transfers between devices with their start and end apart: 1, of which 1 were waited for; matrix products, arithmetic and copies ran while one was open for 1% of the time, Pallas kernels for 0%

commit v1 on v0

v1 whole, which is shorter than its diff:
```python
import functools
import jax
import jax.numpy as jnp
from jax import lax
from jax.experimental import pallas as pl
from jax.experimental.pallas import tpu as pltpu
from jax.sharding import PartitionSpec as P

AXIS = "ep"
RING = 3
MESH_ID = pl.DeviceIdType.MESH
BF16 = jnp.bfloat16
F32 = jnp.float32


def tile_of(size, tile):
    return tile if size % tile == 0 else size


def layer_kernel(n, ids_ref, keep_ref, tok_hbm, wg_hbm, wi_hbm, wo_hbm, out_hbm, back_hbm,
                 tok, ring, recv, wi, wo, hid, acc, buf, wg, frow, col,
                 tok_sem, wg_sem, wi_sem, wo_sem, xs_sem, xr_sem, ys_sem, yr_sem, loc_sem, buf_sem, out_sem):
    tokens, dim = tok.shape
    local_experts, rows, _ = recv.shape
    cap = rows // n
    experts = local_experts * n
    hidden = hid.shape[1]
    me = lax.axis_index(AXIS)
    chips = n // 2
    chip, core = me // 2, lax.rem(me, 2)
    steps = sorted(range(chips), key=lambda d: -min(d, chips - d))
    peers = [lax.rem(chip + step, chips) * 2 + lax.rem(core + other, 2)
             for other in (0, 1) for step in steps if (step, other) != (0, 0)]

    barrier = pltpu.get_barrier_semaphore()
    for peer in peers:
        pl.semaphore_signal(barrier, inc=1, device_id={AXIS: peer}, device_id_type=MESH_ID)

    tok_in = pltpu.make_async_copy(tok_hbm.at[0], tok, tok_sem)
    tok_in.start()
    wg_in = pltpu.make_async_copy(wg_hbm, wg, wg_sem)
    wg_in.start()

    def wi_in(e):
        return pltpu.make_async_copy(wi_hbm.at[e], wi, wi_sem)

    def wo_in(e):
        return pltpu.make_async_copy(wo_hbm.at[e], wo, wo_sem)

    wi_in(0).start()
    wo_in(0).start()

    block = tile_of(tokens, 256)
    tri = (lax.broadcasted_iota(jnp.int32, (block, block), 0)
           < lax.broadcasted_iota(jnp.int32, (block, block), 1)).astype(F32).astype(BF16)
    expert_row = lax.broadcasted_iota(jnp.int32, (experts, tokens), 0)
    first_total = jnp.sum((expert_row == ids_ref[0:1, :]).astype(F32), axis=1, keepdims=True)
    expert_blk = lax.broadcasted_iota(jnp.int32, (experts, block), 0)
    carry_1 = jnp.zeros((experts, 1), F32)
    carry_2 = first_total
    for b in range(tokens // block):
        cols = pl.ds(b * block, block)
        id_1, id_2, keep = ids_ref[0:1, cols], ids_ref[1:2, cols], keep_ref[0:1, cols]
        hot_1 = (expert_blk == id_1).astype(F32)
        hot_2 = jnp.where(expert_blk == id_2, keep.astype(F32), 0.0)
        before = jnp.dot(jnp.concatenate([hot_1, hot_2], axis=0).astype(BF16), tri, preferred_element_type=F32)
        pos_1 = jnp.sum(hot_1 * (before[:experts] + carry_1), axis=0, keepdims=True).astype(jnp.int32)
        pos_2 = jnp.sum(hot_2 * (before[experts:] + carry_2), axis=0, keepdims=True).astype(jnp.int32)
        carry_1 = carry_1 + jnp.sum(hot_1, axis=1, keepdims=True)
        carry_2 = carry_2 + jnp.sum(hot_2, axis=1, keepdims=True)
        frow[0:1, cols] = jnp.where(pos_1 < cap, id_1 * cap + pos_1, -1)
        frow[1:2, cols] = jnp.where((keep == 1) & (pos_2 < cap), id_2 * cap + pos_2, -1)
        frow[2:3, cols] = id_1
        frow[3:4, cols] = id_2
        frow[4:5, cols] = keep
        frow[5:8, cols] = jnp.zeros((3, block), jnp.int32)

    tok_in.wait()
    pl.semaphore_wait(barrier, len(peers))

    n_tile = tile_of(dim, 512)
    h_tile = tile_of(hidden, 512)

    def send_x(e, q):
        peer = peers[q]
        return pltpu.make_async_remote_copy(
            src_ref=ring.at[lax.rem(e, RING), pl.ds(pl.multiple_of(peer * cap, cap), cap)],
            dst_ref=recv.at[e, pl.ds(pl.multiple_of(me * cap, cap), cap)],
            send_sem=xs_sem.at[lax.rem(e, RING), q], recv_sem=xr_sem.at[e, q],
            device_id={AXIS: peer}, device_id_type=MESH_ID)

    def send_y(e, q):
        peer = peers[q]
        return pltpu.make_async_remote_copy(
            src_ref=recv.at[e, pl.ds(pl.multiple_of(peer * cap, cap), cap)],
            dst_ref=back_hbm.at[e, pl.ds(pl.multiple_of(me * cap, cap), cap)],
            send_sem=ys_sem.at[e, q], recv_sem=yr_sem.at[e, q],
            device_id={AXIS: peer}, device_id_type=MESH_ID)

    def own_y(e):
        mine = pl.ds(pl.multiple_of(me * cap, cap), cap)
        return pltpu.make_async_copy(recv.at[e, mine], back_hbm.at[e, mine], loc_sem.at[e])

    def dispatch(e):
        slot = lax.rem(e, RING)

        @pl.loop(0, n)
        def _(d):
            place = lax.broadcasted_iota(jnp.int32, (cap, tokens), 0) + (d * local_experts + e) * cap
            hit = (place == frow[0:1, :]) | (place == frow[1:2, :])
            buf[pl.ds(pl.multiple_of(d * cap, cap), cap), :] = hit.astype(F32).astype(BF16)

        @pl.loop(0, dim // n_tile)
        def _(j):
            cols = pl.ds(pl.multiple_of(j * n_tile, n_tile), n_tile)
            ring[slot, :, cols] = jnp.dot(buf[...], tok[:, cols], preferred_element_type=F32).astype(BF16)

        for q in range(len(peers)):
            send_x(e, q).start()
        mine = pl.ds(pl.multiple_of(me * cap, cap), cap)
        recv[e, mine, :] = ring[slot, mine, :]

    @pl.loop(0, RING)
    def _(e):
        dispatch(e)

    lanes = col.shape[1]
    lane = lax.broadcasted_iota(jnp.int32, (lanes, lanes), 1)
    pad = jnp.zeros((lanes - frow.shape[0], lanes), F32)
    for b in range(tokens // lanes):
        cols = pl.ds(b * lanes, lanes)
        col[cols, :] = jnp.transpose(jnp.concatenate([frow[:, cols].astype(F32), pad], axis=0))
    wg_in.wait()
    g_tile = tile_of(tokens, 512)

    @pl.loop(0, tokens // g_tile)
    def _(b):
        part = pl.ds(pl.multiple_of(b * g_tile, g_tile), g_tile)
        logits = jnp.dot(tok[part, :], wg[...], preferred_element_type=F32)
        grown = jnp.exp(logits - jnp.max(logits, axis=-1, keepdims=True))
        probs = grown / jnp.sum(grown, axis=-1, keepdims=True)
        info = col[part, :]
        expert = lax.broadcasted_iota(jnp.int32, (g_tile, experts), 1).astype(F32)
        gate_1 = jnp.sum(jnp.where(expert == info[:, 2:3], probs, 0.0), axis=-1, keepdims=True)
        gate_2 = jnp.sum(jnp.where(expert == info[:, 3:4], probs * info[:, 4:5], 0.0), axis=-1, keepdims=True)
        total = gate_1 + gate_2
        spot = lax.broadcasted_iota(jnp.int32, (g_tile, lanes), 1)
        col[part, :] = jnp.where(spot == 5, gate_1 / total, jnp.where(spot == 6, gate_2 / total, info))

    m_tile = tile_of(tokens, 512)

    @pl.loop(0, tokens // m_tile)
    def _(b):
        acc[pl.ds(pl.multiple_of(b * m_tile, m_tile), m_tile), :] = jnp.zeros((m_tile, dim), F32)

    def weights(e, part):
        info = col[part, :]
        r = lax.broadcasted_iota(jnp.int32, (1, rows), 1)
        place = (r + (r // cap) * ((local_experts - 1) * cap) + e * cap).astype(F32)
        return jnp.where(place == info[:, 0:1], info[:, 5:6],
                         jnp.where(place == info[:, 1:2], info[:, 6:7], 0.0)).astype(BF16)

    def fetch_back(e):
        for q in range(len(peers)):
            send_y(e, q).wait_recv()
        own_y(e).wait()
        load = pltpu.make_async_copy(back_hbm.at[e], buf, buf_sem)
        load.start()
        load.wait()

    def combine(e, last):
        fetch_back(e)

        @pl.loop(0, tokens // m_tile)
        def _(b):
            part = pl.ds(pl.multiple_of(b * m_tile, m_tile), m_tile)
            mix = weights(e, part)

            @pl.loop(0, dim // n_tile)
            def _(j):
                cols = pl.ds(pl.multiple_of(j * n_tile, n_tile), n_tile)
                value = acc[part, cols] + jnp.dot(mix, buf[:, cols], preferred_element_type=F32)
                if last:
                    tok[part, cols] = value.astype(BF16)
                else:
                    acc[part, cols] = value
            if last:
                pltpu.make_async_copy(tok.at[part], out_hbm.at[part], out_sem.at[b]).start()

    @pl.loop(0, local_experts)
    def _(e):
        for q in range(len(peers)):
            send_x(e, q).wait_recv()
        wi_in(e).wait()

        @pl.loop(0, hidden // h_tile)
        def _(j):
            cols = pl.ds(pl.multiple_of(j * h_tile, h_tile), h_tile)
            hid[:, cols] = jnp.maximum(jnp.dot(recv[e], wi[:, cols], preferred_element_type=F32), 0.0).astype(BF16)

        @pl.when(e + 1 < local_experts)
        def _():
            wi_in(e + 1).start()
        wo_in(e).wait()

        @pl.loop(0, dim // n_tile)
        def _(j):
            cols = pl.ds(pl.multiple_of(j * n_tile, n_tile), n_tile)
            recv[e, :, cols] = jnp.dot(hid[...], wo[:, cols], preferred_element_type=F32).astype(BF16)

        @pl.when(e + 1 < local_experts)
        def _():
            wo_in(e + 1).start()
        for q in range(len(peers)):
            send_y(e, q).start()
        own_y(e).start()

        for q in range(len(peers)):
            send_x(e, q).wait_send()

        @pl.when(e + RING < local_experts)
        def _():
            dispatch(e + RING)

        @pl.when(e >= RING)
        def _():
            combine(e - RING, False)

    @pl.loop(local_experts - RING, local_experts - 1)
    def _(e):
        combine(e, False)

    combine(local_experts - 1, True)

    for b in range(tokens // m_tile):
        part = pl.ds(b * m_tile, m_tile)
        pltpu.make_async_copy(tok.at[part], out_hbm.at[part], out_sem.at[b]).wait()

    @pl.loop(0, local_experts)
    def _(e):
        for q in range(len(peers)):
            send_y(e, q).wait_send()


def solution(mesh):
    n = mesh.shape[AXIS]

    def local_layer(tokens, w_gate, expert_ids, keep_second, w_in, w_out):
        token_count, dim = tokens.shape[1:]
        experts = w_gate.shape[1]
        local_experts, _, hidden = w_in.shape
        cap = 2 * token_count // experts
        rows = n * cap
        out, _ = pl.pallas_call(
            functools.partial(layer_kernel, n),
            out_shape=(jax.ShapeDtypeStruct((token_count, dim), BF16),
                       jax.ShapeDtypeStruct((local_experts, rows, dim), BF16)),
            in_specs=[pl.BlockSpec(memory_space=pltpu.VMEM)] * 2 + [pl.BlockSpec(memory_space=pl.ANY)] * 4,
            out_specs=[pl.BlockSpec(memory_space=pl.ANY)] * 2,
            scratch_shapes=[
                pltpu.VMEM((token_count, dim), BF16),
                pltpu.VMEM((RING, rows, dim), BF16),
                pltpu.VMEM((local_experts, rows, dim), BF16),
                pltpu.VMEM((dim, hidden), BF16),
                pltpu.VMEM((hidden, dim), BF16),
                pltpu.VMEM((rows, hidden), BF16),
                pltpu.VMEM((token_count, dim), F32),
                pltpu.VMEM((rows, dim), BF16),
                pltpu.VMEM((dim, experts), BF16),
                pltpu.VMEM((8, token_count), jnp.int32),
                pltpu.VMEM((token_count, 128), F32),
                pltpu.SemaphoreType.DMA,
                pltpu.SemaphoreType.DMA,
                pltpu.SemaphoreType.DMA,
                pltpu.SemaphoreType.DMA,
                pltpu.SemaphoreType.DMA((RING, n - 1)),
                pltpu.SemaphoreType.DMA((local_experts, n - 1)),
                pltpu.SemaphoreType.DMA((local_experts, n - 1)),
                pltpu.SemaphoreType.DMA((local_experts, n - 1)),
                pltpu.SemaphoreType.DMA((local_experts,)),
                pltpu.SemaphoreType.DMA,
                pltpu.SemaphoreType.DMA((token_count // tile_of(token_count, 512),)),
            ],
            compiler_params=pltpu.CompilerParams(collective_id=0, has_side_effects=True,
                                                 vmem_limit_bytes=67_043_328),
        )(expert_ids[0].T, keep_second, tokens, w_gate, w_in, w_out)
        return out[None]

    group_spec = P(("dp", AXIS))
    return jax.shard_map(local_layer, mesh=mesh, in_specs=(group_spec, P(), group_spec, group_spec, P(AXIS), P(AXIS)), out_specs=group_spec, check_vma=False)
```

time: 598 us -> 398 us (0.67)
  Pallas kernels: 0 us -> 387 us
  blocking collectives: 189 us -> 0 us
  waiting for transfers between devices: 177 us -> 0 us
  matrix products: 160 us -> 0 us
  other arithmetic: 45.8 us -> 0 us
  local copies, waits for them, and re-layouts: 17.8 us -> 10.4 us
  starting transfers between devices: 6.82 us -> 0 us
    pallas_call x0 -> x1, Pallas kernels: none -> 387 us  [local_layer(): pl.pallas_call(functools.partial(layer_kernel, n), out_shape=(jax.ShapeDt...]
    all_to_all x1 -> x0, blocking collectives: 189 us -> none  [local_layer(): recv_rows = lax.all_to_all(send_rows, 'ep', 0, 0, tiled=True)]
    all_to_all x1 -> x0, waiting for transfers between devices: 177 us -> none  [local_layer(): back_rows = lax.all_to_all(back_rows, 'ep', 0, 0, tiled=True)]
    dot_general x5 -> x0, matrix products: 160 us -> none  [the longest x1 51.2 us: local_layer(): jnp.einsum('gsec,ecm->gsm', combine, back_rows, preferred_element_type=jn...]
    another operation x4 -> x0, other arithmetic: 36.6 us -> none
    convert_element_type x1 -> x0, local copies, waits for them, and re-layouts: 14.1 us -> none  [local_layer(): jnp.einsum('egch,ehm->gecm', hidden, w_out, preferred_element_type=jnp.fl...]
    unnamed x30 -> x2, local copies, waits for them, and re-layouts: 1.02 us -> 10.4 us
    all_to_all x1 -> x0, starting transfers between devices: 6.82 us -> none  [local_layer(): back_rows = lax.all_to_all(back_rows, 'ep', 0, 0, tiled=True)]
  transfers between devices with their start and end apart: 1 -> 0, of which waited for: 1 -> 0; matrix products, arithmetic and copies ran while one was open for 1% -> 0% of each run, Pallas kernels for 0% -> 0%
where the time goes in v1:
time: 398 us
  Pallas kernels  387 us (97%)
  local copies, waits for them, and re-layouts  10.4 us (3%)
    pallas_call x1, Pallas kernels, local_layer(): pl.pallas_call(functools.partial(layer_kernel, n), out_shape=(jax.ShapeDt...  387 us
    unnamed x2, local copies, waits for them, and re-layouts  10.4 us

profile of v1, /device:TPU:81, one launch (start us, length us, event | category | flops | bytes accessed | tf_op | source)
XLA Modules:
  0.0 397.8 jit_solution(9015324585661377923)
XLA Ops:
  0.0 2.0 copy.7.wg_hbm
  2.0 387.4 %shard_map.64 = (bf16[2048,2048]{1,0:T(8,128)(2,1)}, bf16[8,512,2048]{2,1,0:T(8,128)(2,1)}) custom-call(s32[2,2048]{1,0:T(2,128)} %bitcast.5, s32[1,2048]{1,0:T(1,128)} %keep_ref.1, bf16[1,2048,2048]{2,1,0:T(8,128)(2,1)} %tok_hbm.1, bf16[2048,64]{1,0:T(8,128)(2,1)} %copy.7.wg_hbm, bf16[8,2048,1024]{2,1,0:T(8,128)(2,1)} %wi_hbm.1, bf16[8,1024,2048]{2,1,0:T(8,128)(2,1)} %wo_hbm.1), custom_call_target="tpu_custom_call" | custom-call | tf_op jit(solution)/shard_map/pallas_call | solution.py:254
  389.4 8.4 %copy.9 = bf16[1,2048,2048]{2,1,0:T(8,128)(2,1)} copy(bf16[1,2048,2048]{2,1,0:T(8,128)(2,1)} %bitcast.4) | data formatting | bytes 16777216

commit v2 on v1

--- a/solution.py
+++ b/solution.py
@@ -17,9 +17,9 @@
     return tile if size % tile == 0 else size
 
 
-def layer_kernel(n, ids_ref, keep_ref, tok_hbm, wg_hbm, wi_hbm, wo_hbm, out_hbm, back_hbm,
-                 tok, ring, recv, wi, wo, hid, acc, buf, wg, frow, col,
-                 tok_sem, wg_sem, wi_sem, wo_sem, xs_sem, xr_sem, ys_sem, yr_sem, loc_sem, buf_sem, out_sem):
+def layer_kernel(n, ids_ref, keep_ref, tok_hbm, wg_hbm, wi_hbm, wo_hbm, tok, back_hbm,
+                 ring, recv, wi, wo, hid, acc, buf, last, wg, frow, col,
+                 tok_sem, wg_sem, wi_sem, wo_sem, xs_sem, xr_sem, ys_sem, yr_sem, yl_sem, loc_sem, buf_sem):
     tokens, dim = tok.shape
     local_experts, rows, _ = recv.shape
     cap = rows // n
@@ -36,8 +36,18 @@
     for peer in peers:
         pl.semaphore_signal(barrier, inc=1, device_id={AXIS: peer}, device_id_type=MESH_ID)
 
-    tok_in = pltpu.make_async_copy(tok_hbm.at[0], tok, tok_sem)
-    tok_in.start()
+    n_tile = tile_of(dim, 512)
+    h_tile = tile_of(hidden, 512)
+    n_count = dim // n_tile
+
+    def n_cols(j):
+        return pl.ds(pl.multiple_of(j * n_tile, n_tile), n_tile)
+
+    def tok_in(j):
+        return pltpu.make_async_copy(tok_hbm.at[0, :, n_cols(j)], tok.at[:, n_cols(j)], tok_sem.at[j])
+
+    for j in range(n_count):
+        tok_in(j).start()
     wg_in = pltpu.make_async_copy(wg_hbm, wg, wg_sem)
     wg_in.start()
 
@@ -46,9 +56,6 @@
 
     def wo_in(e):
         return pltpu.make_async_copy(wo_hbm.at[e], wo, wo_sem)
-
-    wi_in(0).start()
-    wo_in(0).start()
 
     block = tile_of(tokens, 256)
     tri = (lax.broadcasted_iota(jnp.int32, (block, block), 0)
@@ -75,17 +82,11 @@
         frow[4:5, cols] = keep
         frow[5:8, cols] = jnp.zeros((3, block), jnp.int32)
 
-    tok_in.wait()
-    pl.semaphore_wait(barrier, len(peers))
-
-    n_tile = tile_of(dim, 512)
-    h_tile = tile_of(hidden, 512)
-
-    def send_x(e, q):
+    def send_x(e, q, cols=slice(None)):
         peer = peers[q]
         return pltpu.make_async_remote_copy(
-            src_ref=ring.at[lax.rem(e, RING), pl.ds(pl.multiple_of(peer * cap, cap), cap)],
-            dst_ref=recv.at[e, pl.ds(pl.multiple_of(me * cap, cap), cap)],
+            src_ref=ring.at[lax.rem(e, RING), pl.ds(pl.multiple_of(peer * cap, cap), cap), cols],
+            dst_ref=recv.at[e, pl.ds(pl.multiple_of(me * cap, cap), cap), cols],
             send_sem=xs_sem.at[lax.rem(e, RING), q], recv_sem=xr_sem.at[e, q],
             device_id={AXIS: peer}, device_id_type=MESH_ID)
 
@@ -97,30 +98,59 @@
             send_sem=ys_sem.at[e, q], recv_sem=yr_sem.at[e, q],
             device_id={AXIS: peer}, device_id_type=MESH_ID)
 
+    def send_last(j, q):
+        peer = peers[q]
+        return pltpu.make_async_remote_copy(
+            src_ref=recv.at[local_experts - 1, pl.ds(pl.multiple_of(peer * cap, cap), cap), n_cols(j)],
+            dst_ref=last.at[pl.ds(pl.multiple_of(me * cap, cap), cap), n_cols(j)],
+            send_sem=ys_sem.at[local_experts - 1, q], recv_sem=yl_sem.at[j, q],
+            device_id={AXIS: peer}, device_id_type=MESH_ID)
+
     def own_y(e):
         mine = pl.ds(pl.multiple_of(me * cap, cap), cap)
         return pltpu.make_async_copy(recv.at[e, mine], back_hbm.at[e, mine], loc_sem.at[e])
 
-    def dispatch(e):
-        slot = lax.rem(e, RING)
-
+    mine = pl.ds(pl.multiple_of(me * cap, cap), cap)
+
+    def build_mask(e):
         @pl.loop(0, n)
         def _(d):
             place = lax.broadcasted_iota(jnp.int32, (cap, tokens), 0) + (d * local_experts + e) * cap
             hit = (place == frow[0:1, :]) | (place == frow[1:2, :])
             buf[pl.ds(pl.multiple_of(d * cap, cap), cap), :] = hit.astype(F32).astype(BF16)
 
-        @pl.loop(0, dim // n_tile)
+    def dispatch(e):
+        slot = lax.rem(e, RING)
+        build_mask(e)
+
+        @pl.loop(0, n_count)
         def _(j):
-            cols = pl.ds(pl.multiple_of(j * n_tile, n_tile), n_tile)
+            cols = n_cols(j)
             ring[slot, :, cols] = jnp.dot(buf[...], tok[:, cols], preferred_element_type=F32).astype(BF16)
 
         for q in range(len(peers)):
             send_x(e, q).start()
-        mine = pl.ds(pl.multiple_of(me * cap, cap), cap)
         recv[e, mine, :] = ring[slot, mine, :]
 
-    @pl.loop(0, RING)
+    build_mask(0)
+
+    @pl.loop(0, n_count)
+    def _(j):
+        cols = n_cols(j)
+        tok_in(j).wait()
+        ring[0, :, cols] = jnp.dot(buf[...], tok[:, cols], preferred_element_type=F32).astype(BF16)
+
+        @pl.when(j == 0)
+        def _():
+            pl.semaphore_wait(barrier, len(peers))
+        for q in range(len(peers)):
+            send_x(0, q, cols).start()
+        recv[0, mine, cols] = ring[0, mine, cols]
+
+    wi_in(0).start()
+    wo_in(0).start()
+
+    @pl.loop(1, RING)
     def _(e):
         dispatch(e)
 
@@ -136,7 +166,7 @@
     @pl.loop(0, tokens // g_tile)
     def _(b):
         part = pl.ds(pl.multiple_of(b * g_tile, g_tile), g_tile)
-        logits = jnp.dot(tok[part, :], wg[...], preferred_element_type=F32)
+        logits = lax.dot_general(tok[part, :], wg[...], (((1,), (1,)), ((), ())), preferred_element_type=F32)
         grown = jnp.exp(logits - jnp.max(logits, axis=-1, keepdims=True))
         probs = grown / jnp.sum(grown, axis=-1, keepdims=True)
         info = col[part, :]
@@ -147,7 +177,7 @@
         spot = lax.broadcasted_iota(jnp.int32, (g_tile, lanes), 1)
         col[part, :] = jnp.where(spot == 5, gate_1 / total, jnp.where(spot == 6, gate_2 / total, info))
 
-    m_tile = tile_of(tokens, 512)
+    m_tile = rows
 
     @pl.loop(0, tokens // m_tile)
     def _(b):
@@ -168,7 +198,7 @@
         load.start()
         load.wait()
 
-    def combine(e, last):
+    def combine(e):
         fetch_back(e)
 
         @pl.loop(0, tokens // m_tile)
@@ -176,19 +206,12 @@
             part = pl.ds(pl.multiple_of(b * m_tile, m_tile), m_tile)
             mix = weights(e, part)
 
-            @pl.loop(0, dim // n_tile)
+            @pl.loop(0, n_count)
             def _(j):
-                cols = pl.ds(pl.multiple_of(j * n_tile, n_tile), n_tile)
-                value = acc[part, cols] + jnp.dot(mix, buf[:, cols], preferred_element_type=F32)
-                if last:
-                    tok[part, cols] = value.astype(BF16)
-                else:
-                    acc[part, cols] = value
-            if last:
-                pltpu.make_async_copy(tok.at[part], out_hbm.at[part], out_sem.at[b]).start()
-
-    @pl.loop(0, local_experts)
-    def _(e):
+                cols = n_cols(j)
+                acc[part, cols] += jnp.dot(mix, buf[:, cols], preferred_element_type=F32)
+
+    def expert_hidden(e):
         for q in range(len(peers)):
             send_x(e, q).wait_recv()
         wi_in(e).wait()
@@ -198,23 +221,26 @@
             cols = pl.ds(pl.multiple_of(j * h_tile, h_tile), h_tile)
             hid[:, cols] = jnp.maximum(jnp.dot(recv[e], wi[:, cols], preferred_element_type=F32), 0.0).astype(BF16)
 
-        @pl.when(e + 1 < local_experts)
-        def _():
-            wi_in(e + 1).start()
+    def expert_tile(e, j):
+        cols = n_cols(j)
+        recv[e, :, cols] = jnp.dot(hid[...], wo[:, cols], preferred_element_type=F32).astype(BF16)
+
+    final = local_experts - 1
+
+    @pl.loop(0, final)
+    def _(e):
+        expert_hidden(e)
+        wi_in(e + 1).start()
         wo_in(e).wait()
 
-        @pl.loop(0, dim // n_tile)
+        @pl.loop(0, n_count)
         def _(j):
-            cols = pl.ds(pl.multiple_of(j * n_tile, n_tile), n_tile)
-            recv[e, :, cols] = jnp.dot(hid[...], wo[:, cols], preferred_element_type=F32).astype(BF16)
-
-        @pl.when(e + 1 < local_experts)
-        def _():
-            wo_in(e + 1).start()
+            expert_tile(e, j)
+
+        wo_in(e + 1).start()
         for q in range(len(peers)):
             send_y(e, q).start()
         own_y(e).start()
-
         for q in range(len(peers)):
             send_x(e, q).wait_send()
 
@@ -224,17 +250,41 @@
 
         @pl.when(e >= RING)
         def _():
-            combine(e - RING, False)
-
-    @pl.loop(local_experts - RING, local_experts - 1)
+            combine(e - RING)
+
+    expert_hidden(final)
+    wo_in(final).wait()
+
+    @pl.loop(0, n_count)
+    def _(j):
+        expert_tile(final, j)
+        for q in range(len(peers)):
+            send_last(j, q).start()
+        last[mine, n_cols(j)] = recv[final, mine, n_cols(j)]
+
+    for q in range(len(peers)):
+        send_x(final, q).wait_send()
+
+    @pl.loop(final - RING, final)
     def _(e):
-        combine(e, False)
-
-    combine(local_experts - 1, True)
-
-    for b in range(tokens // m_tile):
-        part = pl.ds(b * m_tile, m_tile)
-        pltpu.make_async_copy(tok.at[part], out_hbm.at[part], out_sem.at[b]).wait()
+        combine(e)
+
+    @pl.loop(0, tokens // m_tile)
+    def _(b):
+        part = pl.ds(pl.multiple_of(b * m_tile, m_tile), m_tile)
+        buf[:, pl.ds(pl.multiple_of(b * rows, rows), rows)] = weights(final, part)
+
+    @pl.loop(0, n_count)
+    def _(j):
+        cols = n_cols(j)
+        for q in range(len(peers)):
+            send_last(j, q).wait_recv()
+
+        @pl.loop(0, tokens // m_tile)
+        def _(b):
+            part = pl.ds(pl.multiple_of(b * m_tile, m_tile), m_tile)
+            mix = buf[:, pl.ds(pl.multiple_of(b * rows, rows), rows)]
+            tok[part, cols] = (acc[part, cols] + jnp.dot(mix, last[:, cols], preferred_element_type=F32)).astype(BF16)
 
     @pl.loop(0, local_experts)
     def _(e):
@@ -251,14 +301,14 @@
         local_experts, _, hidden = w_in.shape
         cap = 2 * token_count // experts
         rows = n * cap
-        out, _ = pl.pallas_call(
+        n_count = dim // tile_of(dim, 512)
+        result, _ = pl.pallas_call(
             functools.partial(layer_kernel, n),
-            out_shape=(jax.ShapeDtypeStruct((token_count, dim), BF16),
+            out_shape=(pltpu.VMEM((token_count, dim), BF16),
                        jax.ShapeDtypeStruct((local_experts, rows, dim), BF16)),
             in_specs=[pl.BlockSpec(memory_space=pltpu.VMEM)] * 2 + [pl.BlockSpec(memory_space=pl.ANY)] * 4,
-            out_specs=[pl.BlockSpec(memory_space=pl.ANY)] * 2,
+            out_specs=[pl.BlockSpec(memory_space=pltpu.VMEM), pl.BlockSpec(memory_space=pl.ANY)],
             scratch_shapes=[
-                pltpu.VMEM((token_count, dim), BF16),
                 pltpu.VMEM((RING, rows, dim), BF16),
                 pltpu.VMEM((local_experts, rows, dim), BF16),
                 pltpu.VMEM((dim, hidden), BF16),
@@ -266,10 +316,11 @@
                 pltpu.VMEM((rows, hidden), BF16),
                 pltpu.VMEM((token_count, dim), F32),
                 pltpu.VMEM((rows, dim), BF16),
-                pltpu.VMEM((dim, experts), BF16),
+                pltpu.VMEM((rows, dim), BF16),
+                pltpu.VMEM((experts, dim), BF16),
                 pltpu.VMEM((8, token_count), jnp.int32),
                 pltpu.VMEM((token_count, 128), F32),
-                pltpu.SemaphoreType.DMA,
+                pltpu.SemaphoreType.DMA((n_count,)),
                 pltpu.SemaphoreType.DMA,
                 pltpu.SemaphoreType.DMA,
                 pltpu.SemaphoreType.DMA,
@@ -277,14 +328,14 @@
                 pltpu.SemaphoreType.DMA((local_experts, n - 1)),
                 pltpu.SemaphoreType.DMA((local_experts, n - 1)),
                 pltpu.SemaphoreType.DMA((local_experts, n - 1)),
+                pltpu.SemaphoreType.DMA((n_count, n - 1)),
                 pltpu.SemaphoreType.DMA((local_experts,)),
                 pltpu.SemaphoreType.DMA,
-                pltpu.SemaphoreType.DMA((token_count // tile_of(token_count, 512),)),
             ],
             compiler_params=pltpu.CompilerParams(collective_id=0, has_side_effects=True,
-                                                 vmem_limit_bytes=67_043_328),
-        )(expert_ids[0].T, keep_second, tokens, w_gate, w_in, w_out)
-        return out[None]
+                                                 vmem_limit_bytes=58_195_968),
+        )(expert_ids[0].T, keep_second, tokens, w_gate.T, w_in, w_out)
+        return result[None]
 
     group_spec = P(("dp", AXIS))
     return jax.shard_map(local_layer, mesh=mesh, in_specs=(group_spec, P(), group_spec, group_spec, P(AXIS), P(AXIS)), out_specs=group_spec, check_vma=False)

time: 398 us -> 376 us (0.945)
  Pallas kernels: 387 us -> 372 us
  local copies, waits for them, and re-layouts: 10.4 us -> 3.4 us
    pallas_call x1, Pallas kernels: 387 us -> 372 us  [local_layer(): pl.pallas_call(functools.partial(layer_kernel, n), out_shape=(pltpu.VMEM(...]
    unnamed x2 -> x1, local copies, waits for them, and re-layouts: 10.4 us -> 3.4 us
where the time goes in v2:
time: 376 us; the launch traced here: 375 us
  Pallas kernels  372 us (99%)
    pallas_call x1, Pallas kernels, local_layer(): pl.pallas_call(functools.partial(layer_kernel, n), out_shape=(pltpu.VMEM(...  372 us

profile of v2, /device:TPU:81, one launch (start us, length us, event | category | flops | bytes accessed | tf_op | source)
XLA Modules:
  0.0 375.4 jit_solution(12636635454107129709)
XLA Ops:
  0.0 372.0 %shard_map.64 = (bf16[2048,2048]{1,0:T(8,128)(2,1)S(1)}, bf16[8,512,2048]{2,1,0:T(8,128)(2,1)}) custom-call(s32[2,2048]{1,0:T(2,128)} %bitcast.7, s32[1,2048]{1,0:T(1,128)} %keep_ref.1, bf16[1,2048,2048]{2,1,0:T(8,128)(2,1)} %tok_hbm.1, bf16[64,2048]{1,0:T(8,128)(2,1)} %bitcast.6, bf16[8,2048,1024]{2,1,0:T(8,128)(2,1)} %wi_hbm.1, bf16[8,1024,2048]{2,1,0:T(8,128)(2,1)} %wo_hbm.1), custom_call_target="tpu_custom_call" | custom-call | tf_op jit(solution)/shard_map/pallas_call | solution.py:305
  372.0 3.4 copy.8

commit v3 on v2

--- a/solution.py
+++ b/solution.py
@@ -17,9 +17,9 @@
     return tile if size % tile == 0 else size
 
 
-def layer_kernel(n, ids_ref, keep_ref, tok_hbm, wg_hbm, wi_hbm, wo_hbm, tok, back_hbm,
-                 ring, recv, wi, wo, hid, acc, buf, last, wg, frow, col,
-                 tok_sem, wg_sem, wi_sem, wo_sem, xs_sem, xr_sem, ys_sem, yr_sem, yl_sem, loc_sem, buf_sem):
+def layer_kernel(n, ids_hbm, keep_hbm, tok_hbm, wg_hbm, wi_hbm, wo_hbm, tok, back_hbm,
+                 ring, recv, wi, wo, hid, acc, buf, last, wg, ids_ref, keep_ref, frow, col,
+                 tok_sem, ids_sem, wg_sem, wi_sem, wo_sem, xs_sem, xr_sem, ys_sem, yr_sem, yl_sem, loc_sem, buf_sem):
     tokens, dim = tok.shape
     local_experts, rows, _ = recv.shape
     cap = rows // n
@@ -43,19 +43,31 @@
     def n_cols(j):
         return pl.ds(pl.multiple_of(j * n_tile, n_tile), n_tile)
 
-    def tok_in(j):
-        return pltpu.make_async_copy(tok_hbm.at[0, :, n_cols(j)], tok.at[:, n_cols(j)], tok_sem.at[j])
-
-    for j in range(n_count):
-        tok_in(j).start()
+    edge = tile_of(n_tile, 256)
+    head_cols = [pl.ds(0, edge)] + [pl.ds(edge, n_tile - edge)] * (edge < n_tile)
+    tail_cols = [pl.ds(dim - n_tile, n_tile - edge)] * (edge < n_tile) + [pl.ds(dim - edge, edge)]
+    heads = len(head_cols) - 1
+
+    def tok_in(j, cols):
+        return pltpu.make_async_copy(tok_hbm.at[0, :, cols], tok.at[:, cols], tok_sem.at[j])
+
+    ids_in = pltpu.make_async_copy(ids_hbm, ids_ref, ids_sem.at[0])
+    keep_in = pltpu.make_async_copy(keep_hbm, keep_ref, ids_sem.at[1])
     wg_in = pltpu.make_async_copy(wg_hbm, wg, wg_sem)
-    wg_in.start()
+    ids_in.start()
+    keep_in.start()
+    tok_in(0, head_cols[0]).start()
 
     def wi_in(e):
         return pltpu.make_async_copy(wi_hbm.at[e], wi, wi_sem)
 
     def wo_in(e):
         return pltpu.make_async_copy(wo_hbm.at[e], wo, wo_sem)
+
+    ids_in.wait()
+    keep_in.wait()
+    for j in range(1, heads + 1):
+        tok_in(j, head_cols[j]).start()
 
     block = tile_of(tokens, 256)
     tri = (lax.broadcasted_iota(jnp.int32, (block, block), 0)
@@ -87,7 +99,7 @@
         return pltpu.make_async_remote_copy(
             src_ref=ring.at[lax.rem(e, RING), pl.ds(pl.multiple_of(peer * cap, cap), cap), cols],
             dst_ref=recv.at[e, pl.ds(pl.multiple_of(me * cap, cap), cap), cols],
-            send_sem=xs_sem.at[lax.rem(e, RING), q], recv_sem=xr_sem.at[e, q],
+            send_sem=xs_sem.at[lax.rem(e, RING)], recv_sem=xr_sem.at[e],
             device_id={AXIS: peer}, device_id_type=MESH_ID)
 
     def send_y(e, q):
@@ -95,20 +107,25 @@
         return pltpu.make_async_remote_copy(
             src_ref=recv.at[e, pl.ds(pl.multiple_of(peer * cap, cap), cap)],
             dst_ref=back_hbm.at[e, pl.ds(pl.multiple_of(me * cap, cap), cap)],
-            send_sem=ys_sem.at[e, q], recv_sem=yr_sem.at[e, q],
+            send_sem=ys_sem.at[e], recv_sem=yr_sem.at[e],
             device_id={AXIS: peer}, device_id_type=MESH_ID)
 
-    def send_last(j, q):
+    def send_last(j, cols, q):
         peer = peers[q]
         return pltpu.make_async_remote_copy(
-            src_ref=recv.at[local_experts - 1, pl.ds(pl.multiple_of(peer * cap, cap), cap), n_cols(j)],
-            dst_ref=last.at[pl.ds(pl.multiple_of(me * cap, cap), cap), n_cols(j)],
-            send_sem=ys_sem.at[local_experts - 1, q], recv_sem=yl_sem.at[j, q],
+            src_ref=recv.at[local_experts - 1, pl.ds(pl.multiple_of(peer * cap, cap), cap), cols],
+            dst_ref=last.at[pl.ds(pl.multiple_of(me * cap, cap), cap), cols],
+            send_sem=ys_sem.at[local_experts - 1], recv_sem=yl_sem.at[j],
             device_id={AXIS: peer}, device_id_type=MESH_ID)
+
+    away = pl.ds(0, len(peers) * cap)
+
+    def wait_all(sem, cols=slice(None)):
+        pltpu.make_async_copy(back_hbm.at[0, away, cols], last.at[away, cols], sem).wait()
 
     def own_y(e):
         mine = pl.ds(pl.multiple_of(me * cap, cap), cap)
-        return pltpu.make_async_copy(recv.at[e, mine], back_hbm.at[e, mine], loc_sem.at[e])
+        return pltpu.make_async_copy(recv.at[e, mine], back_hbm.at[e, mine], loc_sem)
 
     mine = pl.ds(pl.multiple_of(me * cap, cap), cap)
 
@@ -133,22 +150,30 @@
         recv[e, mine, :] = ring[slot, mine, :]
 
     build_mask(0)
-
-    @pl.loop(0, n_count)
-    def _(j):
-        cols = n_cols(j)
-        tok_in(j).wait()
-        ring[0, :, cols] = jnp.dot(buf[...], tok[:, cols], preferred_element_type=F32).astype(BF16)
-
-        @pl.when(j == 0)
-        def _():
+    for j in range(1, n_count):
+        tok_in(heads + j, n_cols(j)).start()
+
+    def first_out(j, cols):
+        tok_in(j, cols).wait()
+        half = rows // 2
+        for h in (pl.ds(0, half), pl.ds(half, half)):
+            ring[0, h, cols] = jnp.dot(buf[h, :], tok[:, cols], preferred_element_type=F32).astype(BF16)
+        if isinstance(j, int) and j == 0:
             pl.semaphore_wait(barrier, len(peers))
         for q in range(len(peers)):
             send_x(0, q, cols).start()
         recv[0, mine, cols] = ring[0, mine, cols]
 
+    for j, cols in enumerate(head_cols):
+        first_out(j, cols)
+
+    @pl.loop(1, n_count)
+    def _(j):
+        first_out(j + heads, n_cols(j))
+
     wi_in(0).start()
     wo_in(0).start()
+    wg_in.start()
 
     @pl.loop(1, RING)
     def _(e):
@@ -191,9 +216,7 @@
                          jnp.where(place == info[:, 1:2], info[:, 6:7], 0.0)).astype(BF16)
 
     def fetch_back(e):
-        for q in range(len(peers)):
-            send_y(e, q).wait_recv()
-        own_y(e).wait()
+        wait_all(yr_sem.at[e])
         load = pltpu.make_async_copy(back_hbm.at[e], buf, buf_sem)
         load.start()
         load.wait()
@@ -212,8 +235,7 @@
                 acc[part, cols] += jnp.dot(mix, buf[:, cols], preferred_element_type=F32)
 
     def expert_hidden(e):
-        for q in range(len(peers)):
-            send_x(e, q).wait_recv()
+        wait_all(xr_sem.at[e])
         wi_in(e).wait()
 
         @pl.loop(0, hidden // h_tile)
@@ -221,8 +243,7 @@
             cols = pl.ds(pl.multiple_of(j * h_tile, h_tile), h_tile)
             hid[:, cols] = jnp.maximum(jnp.dot(recv[e], wi[:, cols], preferred_element_type=F32), 0.0).astype(BF16)
 
-    def expert_tile(e, j):
-        cols = n_cols(j)
+    def expert_tile(e, cols):
         recv[e, :, cols] = jnp.dot(hid[...], wo[:, cols], preferred_element_type=F32).astype(BF16)
 
     final = local_experts - 1
@@ -235,19 +256,20 @@
 
         @pl.loop(0, n_count)
         def _(j):
-            expert_tile(e, j)
+            expert_tile(e, n_cols(j))
 
         wo_in(e + 1).start()
         for q in range(len(peers)):
             send_y(e, q).start()
         own_y(e).start()
-        for q in range(len(peers)):
-            send_x(e, q).wait_send()
+        wait_all(xs_sem.at[lax.rem(e, RING)])
 
         @pl.when(e + RING < local_experts)
         def _():
             dispatch(e + RING)
 
+        own_y(e).wait()
+
         @pl.when(e >= RING)
         def _():
             combine(e - RING)
@@ -255,15 +277,20 @@
     expert_hidden(final)
     wo_in(final).wait()
 
-    @pl.loop(0, n_count)
+    def last_out(j, cols):
+        expert_tile(final, cols)
+        for q in range(len(peers)):
+            send_last(j, cols, q).start()
+        last[mine, cols] = recv[final, mine, cols]
+
+    @pl.loop(0, n_count - 1)
     def _(j):
-        expert_tile(final, j)
-        for q in range(len(peers)):
-            send_last(j, q).start()
-        last[mine, n_cols(j)] = recv[final, mine, n_cols(j)]
-
-    for q in range(len(peers)):
-        send_x(final, q).wait_send()
+        last_out(j, n_cols(j))
+
+    for k, cols in enumerate(tail_cols):
+        last_out(n_count - 1 + k, cols)
+
+    wait_all(xs_sem.at[final % RING])
 
     @pl.loop(final - RING, final)
     def _(e):
@@ -274,22 +301,24 @@
         part = pl.ds(pl.multiple_of(b * m_tile, m_tile), m_tile)
         buf[:, pl.ds(pl.multiple_of(b * rows, rows), rows)] = weights(final, part)
 
-    @pl.loop(0, n_count)
+    def last_in(j, cols):
+        wait_all(yl_sem.at[j], cols)
+
+        for b in range(tokens // m_tile):
+            part = pl.ds(b * m_tile, m_tile)
+            mix = buf[:, pl.ds(b * rows, rows)]
+            tok[part, cols] = (acc[part, cols] + jnp.dot(mix, last[:, cols], preferred_element_type=F32)).astype(BF16)
+
+    @pl.loop(0, n_count - 1)
     def _(j):
-        cols = n_cols(j)
-        for q in range(len(peers)):
-            send_last(j, q).wait_recv()
-
-        @pl.loop(0, tokens // m_tile)
-        def _(b):
-            part = pl.ds(pl.multiple_of(b * m_tile, m_tile), m_tile)
-            mix = buf[:, pl.ds(pl.multiple_of(b * rows, rows), rows)]
-            tok[part, cols] = (acc[part, cols] + jnp.dot(mix, last[:, cols], preferred_element_type=F32)).astype(BF16)
+        last_in(j, n_cols(j))
+
+    for k, cols in enumerate(tail_cols):
+        last_in(n_count - 1 + k, cols)
 
     @pl.loop(0, local_experts)
     def _(e):
-        for q in range(len(peers)):
-            send_y(e, q).wait_send()
+        wait_all(ys_sem.at[e])
 
 
 def solution(mesh):
@@ -306,7 +335,7 @@
             functools.partial(layer_kernel, n),
             out_shape=(pltpu.VMEM((token_count, dim), BF16),
                        jax.ShapeDtypeStruct((local_experts, rows, dim), BF16)),
-            in_specs=[pl.BlockSpec(memory_space=pltpu.VMEM)] * 2 + [pl.BlockSpec(memory_space=pl.ANY)] * 4,
+            in_specs=[pl.BlockSpec(memory_space=pl.ANY)] * 6,
             out_specs=[pl.BlockSpec(memory_space=pltpu.VMEM), pl.BlockSpec(memory_space=pl.ANY)],
             scratch_shapes=[
                 pltpu.VMEM((RING, rows, dim), BF16),
@@ -318,18 +347,21 @@
                 pltpu.VMEM((rows, dim), BF16),
                 pltpu.VMEM((rows, dim), BF16),
                 pltpu.VMEM((experts, dim), BF16),
+                pltpu.VMEM((2, token_count), jnp.int32),
+                pltpu.VMEM((1, token_count), jnp.int32),
                 pltpu.VMEM((8, token_count), jnp.int32),
                 pltpu.VMEM((token_count, 128), F32),
-                pltpu.SemaphoreType.DMA((n_count,)),
-                pltpu.SemaphoreType.DMA,
-                pltpu.SemaphoreType.DMA,
-                pltpu.SemaphoreType.DMA,
-                pltpu.SemaphoreType.DMA((RING, n - 1)),
-                pltpu.SemaphoreType.DMA((local_experts, n - 1)),
-                pltpu.SemaphoreType.DMA((local_experts, n - 1)),
-                pltpu.SemaphoreType.DMA((local_experts, n - 1)),
-                pltpu.SemaphoreType.DMA((n_count, n - 1)),
+                pltpu.SemaphoreType.DMA((n_count + 1,)),
+                pltpu.SemaphoreType.DMA((2,)),
+                pltpu.SemaphoreType.DMA,
+                pltpu.SemaphoreType.DMA,
+                pltpu.SemaphoreType.DMA,
+                pltpu.SemaphoreType.DMA((RING,)),
                 pltpu.SemaphoreType.DMA((local_experts,)),
+                pltpu.SemaphoreType.DMA((local_experts,)),
+                pltpu.SemaphoreType.DMA((local_experts,)),
+                pltpu.SemaphoreType.DMA((n_count + 1,)),
+                pltpu.SemaphoreType.DMA,
                 pltpu.SemaphoreType.DMA,
             ],
             compiler_params=pltpu.CompilerParams(collective_id=0, has_side_effects=True,

time: 376 us -> 372 us (0.989)
  Pallas kernels: 372 us -> 368 us
    pallas_call x1, Pallas kernels: 372 us -> 368 us  [local_layer(): pl.pallas_call(functools.partial(layer_kernel, n), out_shape=(pltpu.VMEM(...]
where the time goes in v3:
time: 372 us; the launch traced here: 371 us
  Pallas kernels  368 us (99%)
    pallas_call x1, Pallas kernels, local_layer(): pl.pallas_call(functools.partial(layer_kernel, n), out_shape=(pltpu.VMEM(...  368 us

profile of v3, /device:TPU:81, one launch (start us, length us, event | category | flops | bytes accessed | tf_op | source)
XLA Modules:
  0.0 371.5 jit_solution(16079566054030753320)
XLA Ops:
  0.0 368.1 %shard_map.64 = (bf16[2048,2048]{1,0:T(8,128)(2,1)S(1)}, bf16[8,512,2048]{2,1,0:T(8,128)(2,1)}) custom-call(s32[2,2048]{1,0:T(2,128)} %bitcast.7, s32[1,2048]{1,0:T(1,128)} %keep_hbm.1, bf16[1,2048,2048]{2,1,0:T(8,128)(2,1)} %tok_hbm.1, bf16[64,2048]{1,0:T(8,128)(2,1)} %bitcast.6, bf16[8,2048,1024]{2,1,0:T(8,128)(2,1)} %wi_hbm.1, bf16[8,1024,2048]{2,1,0:T(8,128)(2,1)} %wo_hbm.1), custom_call_target="tpu_custom_call" | custom-call | tf_op jit(solution)/shard_map/pallas_call | solution.py:334
  368.1 3.4 copy.8

commit v4 on v3

--- a/solution.py
+++ b/solution.py
@@ -31,6 +31,8 @@
     steps = sorted(range(chips), key=lambda d: -min(d, chips - d))
     peers = [lax.rem(chip + step, chips) * 2 + lax.rem(core + other, 2)
              for other in (0, 1) for step in steps if (step, other) != (0, 0)]
+
+    peer_steps = [step for other in (0, 1) for step in steps if (step, other) != (0, 0)]
 
     barrier = pltpu.get_barrier_semaphore()
     for peer in peers:
@@ -155,13 +157,20 @@
 
     def first_out(j, cols):
         tok_in(j, cols).wait()
-        half = rows // 2
-        for h in (pl.ds(0, half), pl.ds(half, half)):
-            ring[0, h, cols] = jnp.dot(buf[h, :], tok[:, cols], preferred_element_type=F32).astype(BF16)
-        if isinstance(j, int) and j == 0:
-            pl.semaphore_wait(barrier, len(peers))
-        for q in range(len(peers)):
-            send_x(0, q, cols).start()
+        parts = steps if isinstance(j, int) and j == 0 else (0,)
+        for k, step in enumerate(parts):
+            size = rows // len(parts)
+            spot = pl.ds(pl.multiple_of(lax.rem(chip + step, len(parts)) * size, size), size)
+            ring[0, spot, cols] = jnp.dot(buf[spot, :], tok[:, cols], preferred_element_type=F32).astype(BF16)
+            if len(parts) > 1:
+                if k == 0:
+                    pl.semaphore_wait(barrier, len(peers))
+                for q in range(len(peers)):
+                    if peer_steps[q] == step:
+                        send_x(0, q, cols).start()
+        if len(parts) == 1:
+            for q in range(len(peers)):
+                send_x(0, q, cols).start()
         recv[0, mine, cols] = ring[0, mine, cols]
 
     for j, cols in enumerate(head_cols):

time: 372 us -> 371 us (level)
  no operation moved by 1% of the time
where the time goes in v4:
time: 371 us
  Pallas kernels  368 us (99%)
    pallas_call x1, Pallas kernels, local_layer(): pl.pallas_call(functools.partial(layer_kernel, n), out_shape=(pltpu.VMEM(...  368 us

profile of v4, /device:TPU:81, one launch (start us, length us, event | category | flops | bytes accessed | tf_op | source)
XLA Modules:
  0.0 371.2 jit_solution(17456547801105272613)
XLA Ops:
  0.0 367.8 %shard_map.64 = (bf16[2048,2048]{1,0:T(8,128)(2,1)S(1)}, bf16[8,512,2048]{2,1,0:T(8,128)(2,1)}) custom-call(s32[2,2048]{1,0:T(2,128)} %bitcast.7, s32[1,2048]{1,0:T(1,128)} %keep_hbm.1, bf16[1,2048,2048]{2,1,0:T(8,128)(2,1)} %tok_hbm.1, bf16[64,2048]{1,0:T(8,128)(2,1)} %bitcast.6, bf16[8,2048,1024]{2,1,0:T(8,128)(2,1)} %wi_hbm.1, bf16[8,1024,2048]{2,1,0:T(8,128)(2,1)} %wo_hbm.1), custom_call_target="tpu_custom_call" | custom-call | tf_op jit(solution)/shard_map/pallas_call | solution.py:343
  367.8 3.4 copy.8
